TPU v7x, 128 devices: a whole 4x4x4 slice. The times are simulated.
128 devices in a mesh: blk: 32 (over x, z, core), grp: 4 (over y).
Axes of the slice: x: 4, y: 4, z: 4, core: 2. Of those that a mesh axis runs over, the one named last changes fastest.
Arguments:
- statistics: float32 [4, 64, 512, 512], P('grp', 'blk'), as said below
- gradients: bfloat16 [4, 16, 512, 14336], P('grp', None, None, 'blk'), may hold values from -6 to 6
- live_counts: int32 [4, 32], P('grp'), may hold values from 0 to 2, as said below
- slot_row: int32 [4, 64], P('grp'), may hold values from 0 to 15, as said below
- sweeps: int32 [4, 64], P('grp', 'blk'), may hold values from 1 to 2, as said below
Outputs:
- updates: bfloat16 [4, 16, 512, 14336], P('grp', None, None, 'blk')
- off_max: float32 [2], replicated
Inputs may be any that keep to these rules, and one draw needn't show every extreme that they name: `live_counts`: the live slots of one index of grp number exactly 16; in every draw some device of each grp index has 2 live slots. `slot_row`: over the live slots of one index of grp each row block 0 to 15 appears exactly once. In each index of grp some live slot has 2 sweeps. `statistics`: every block is symmetric positive definite.
All inputs are finite; a program needn't handle non-finite values.
Results may differ from a plain program's by a relative error of at most 0.0051.
Values may be sent and summed in bfloat16 or wider, within the bound.
No kernel may reach another device: no remote copies, remote signals or barrier semaphores. Data moves between devices by JAX's collectives and lax.ppermute only.
A program may use at most 192 MiB of HBM per device.

v0:
```python
import functools

import jax
import jax.numpy as jnp
from jax import lax
from jax.sharding import Mesh
from jax.sharding import PartitionSpec as P

MAXS = 2
BLK = ("blk_0", "blk_1", "blk_2")
BLK_GRP = ("blk_0", "blk_1", "blk_2", "grp")


damping = 0.01
pairings = ((0, 1, 2, 3), (0, 2, 1, 3), (0, 3, 1, 2))
highest = lax.Precision.HIGHEST


def by_axis(x, axes):
    return functools.reduce(lax.pmax, axes, x)


def regroup_cols(values, pairing, group_width):
    return jnp.concatenate(
        [values[:, member * group_width : (member + 1) * group_width] for member in pairing], axis=1
    )


def regroup(values, pairing, group_width):
    stacked = jnp.concatenate(
        [values[member * group_width : (member + 1) * group_width] for member in pairing], axis=0
    )
    return regroup_cols(stacked, pairing, group_width)


def angle_block(square_sub):
    group_width = square_sub.shape[-1] // 2
    diagonal = jnp.diagonal(square_sub, axis1=1, axis2=2)
    lower_diag = diagonal[:, :group_width, None]
    upper_diag = diagonal[:, None, group_width:]
    coupling = square_sub[:, :group_width, group_width:]
    difference = upper_diag - lower_diag
    bottom = (
        difference * difference
        + 4.0 * coupling * coupling
        + damping * (lower_diag + upper_diag) ** 2
    )
    return coupling * difference / bottom


def rotation_of(square_sub):
    angles = angle_block(square_sub)
    group_width = angles.shape[-1]
    identity = jnp.eye(group_width, dtype=jnp.float32)
    outer = jnp.einsum("hpq,hrq->hpr", angles, angles, precision=highest)
    inner = jnp.einsum("hqp,hqr->hpr", angles, angles, precision=highest)
    left_factor = jnp.linalg.cholesky(identity + 0.25 * outer)
    right_factor = jnp.linalg.cholesky(identity + 0.25 * inner)
    top_rows = jnp.concatenate([identity - 0.25 * outer, angles], axis=2)
    low_rows = jnp.concatenate([-jnp.swapaxes(angles, 1, 2), identity - 0.25 * inner], axis=2)
    top_half = jax.scipy.linalg.cho_solve((left_factor, True), top_rows)
    low_half = jax.scipy.linalg.cho_solve((right_factor, True), low_rows)
    return jnp.concatenate([top_half, low_half], axis=1)


def rotate_round(matrix, vectors, pairing):
    block_size = matrix.shape[0]
    group_width = block_size // 4
    restore = [pairing.index(member) for member in range(4)]
    matrix = regroup(matrix, pairing, group_width)
    vectors = regroup_cols(vectors, pairing, group_width)
    half_size = 2 * group_width
    square_sub = jnp.stack([matrix[:half_size, :half_size], matrix[half_size:, half_size:]])
    rotation = rotation_of(square_sub)
    row_part = jnp.einsum(
        "hpq,hpc->hqc", rotation, matrix.reshape(2, half_size, block_size), precision=highest
    )
    row_part = row_part.reshape(block_size, block_size)
    matrix = jnp.einsum(
        "rhp,hpq->rhq", row_part.reshape(block_size, 2, half_size), rotation, precision=highest
    )
    matrix = matrix.reshape(block_size, block_size)
    vectors = jnp.einsum(
        "rhp,hpq->rhq", vectors.reshape(block_size, 2, half_size), rotation, precision=highest
    )
    vectors = vectors.reshape(block_size, block_size)
    return (regroup(matrix, restore, group_width), regroup_cols(vectors, restore, group_width))


def one_sweep(matrix, vectors):
    for pairing in pairings:
        matrix, vectors = rotate_round(matrix, vectors, pairing)
    return (matrix, vectors)


def keep_both(matrix, vectors):
    return (matrix, vectors)


def off_norm(matrix):
    block_size = matrix.shape[0]
    on_diagonal = lax.broadcasted_iota(
        jnp.int32, (block_size, block_size), 0
    ) == lax.broadcasted_iota(jnp.int32, (block_size, block_size), 1)
    outside = jnp.where(on_diagonal, 0.0, matrix)
    return jnp.sqrt(jnp.sum(outside * outside) / jnp.sum(matrix * matrix))


def root_factor(matrix, vectors):
    scales = jnp.power(jnp.diagonal(matrix), -0.25)
    return jnp.dot(vectors * scales[None, :], vectors.T, precision=highest).astype(jnp.bfloat16)


def per_device(statistics, gradients, live_counts, slot_row, sweeps):
    matrices = statistics[0]
    slot_count = matrices.shape[0]
    block_size = matrices.shape[1]
    row_count = gradients.shape[1]
    blk_rank = lax.axis_index(BLK)
    own_live = lax.dynamic_index_in_dim(live_counts[0], blk_rank, 0, keepdims=False)
    own_sweeps = sweeps[0]
    identity = jnp.eye(block_size, dtype=jnp.float32)
    states = [matrices[slot_index] for slot_index in range(slot_count)]
    eigen_bases = [identity for slot_index in range(slot_count)]
    live_flags = [slot_index < own_live for slot_index in range(slot_count)]
    sweep_list = [own_sweeps[slot_index] for slot_index in range(slot_count)]
    local_peaks = jnp.zeros((MAXS,), jnp.float32)
    for slot_index in range(slot_count):
        for sweep_index in range(MAXS):
            active = jnp.logical_and(live_flags[slot_index], sweep_list[slot_index] > sweep_index)
            states[slot_index], eigen_bases[slot_index] = lax.cond(
                active, one_sweep, keep_both, states[slot_index], eigen_bases[slot_index]
            )
            local_peaks = local_peaks.at[sweep_index].max(
                jnp.where(active, off_norm(states[slot_index]), jnp.float32(0.0))
            )
    off_max = by_axis(local_peaks, BLK_GRP)
    blank_factor = jnp.zeros((block_size, block_size), jnp.bfloat16)
    factor_list = [
        jnp.where(
            live_flags[slot_index],
            root_factor(states[slot_index], eigen_bases[slot_index]),
            blank_factor,
        )
        for slot_index in range(slot_count)
    ]
    factors = jnp.stack(factor_list)
    row_ids = lax.iota(jnp.int32, row_count)
    gathered = lax.all_gather(factors, BLK, axis=0, tiled=True)
    slot_total = gathered.shape[0]
    slot_ids = lax.iota(jnp.int32, slot_total)
    is_live = slot_ids % slot_count < jnp.repeat(live_counts[0], slot_count)
    matches = (slot_row[0][None, :] == row_ids[:, None]) & is_live[None, :]
    slot_of = jnp.sum(jnp.where(matches, slot_ids[None, :], 0), axis=1)
    chosen = jnp.take(gathered, slot_of, axis=0)
    updates = jnp.einsum("kij,kjc->kic", chosen, gradients[0], preferred_element_type=jnp.float32)
    return (updates.astype(jnp.bfloat16)[None], off_max)


def solution(mesh):
    split = Mesh(
        mesh.devices.reshape(4, 4, 2, mesh.shape["grp"]), ("blk_0", "blk_1", "blk_2", "grp")
    )
    return jax.shard_map(
        per_device,
        mesh=split,
        in_specs=(
            P("grp", BLK, None, None),
            P("grp", None, None, BLK),
            P("grp", None),
            P("grp", None),
            P("grp", BLK),
        ),
        out_specs=(P("grp", None, None, BLK), P()),
        check_vma=False,
    )
```

profile of v0, /device:TPU:1, one launch (start us, length us, event | category | flops | bytes accessed | tf_op | source)
XLA Modules:
  0.0 1781.5 jit_solution(11419021902682509797)
XLA Ops:
  7.2 1.3 fusion.482
  11.3 1.2 fusion.483
  14.5 2.7 slice_bitcast_fusion.9
  17.2 8.5 conditional.4
  17.2 0.3 copy.1039
  25.6 1.3 copy.1042
  27.0 1.3 copy.1041
  28.3 15.3 conditional.5
  28.3 1.0 copy.1241
  43.6 8.9 gather_fusion.12
  52.5 10.5 conditional.6
  52.5 2.5 copy.1043
  63.1 1.3 copy.1046
  64.4 2.5 copy.1045
  66.9 11.1 conditional.7
  66.9 2.3 copy.1233
  78.0 8.5 gather_fusion.13
  86.6 2.0 fusion.416
  88.5 2.6 fusion.410
  91.2 1.1 pad_maximum_fusion.116
  92.2 2.2 multiply_reduce_fusion.3
  95.8 0.9 multiply_reduce_fusion.6
  98.2 2.2 multiply_reduce_fusion.1
  101.8 2.2 multiply_reduce_fusion
  105.6 9.3 pmax.28
  114.9 767.3 %pmax.29 = f32[2]{0:T(128)S(1)} all-reduce(f32[2]{0:T(128)S(1)} %pmax.28), channel_id=1, replica_groups=mesh['blk_0'=4,'blk_1'=4,'blk_2'=2,'grp'=4] {'blk_1'}, use_global_device_ids=true, to_apply=%region_20.23 | all-reduce | flops 2 | bytes 16 | tf_op jit(solution)/shard_map/pmax | solution.py:20
  882.2 794.6 %pmax.30 = f32[2]{0:T(128)S(1)} all-reduce(f32[2]{0:T(128)S(1)} %pmax.29), channel_id=1, replica_groups=mesh['blk_0'=4,'blk_1'=4,'blk_2'=2,'grp'=4] {'blk_2'}, use_global_device_ids=true, to_apply=%region_21.24 | all-reduce | flops 2 | bytes 16 | tf_op jit(solution)/shard_map/pmax | solution.py:20
  1676.8 11.6 pmax.31
  1688.7 0.8 select_reduce_fusion.24
  1689.5 68.1 %all-gather.2.cloned.1.call-done = bf16[64,512,512]{2,1,0:T(8,128)(2,1)} async-done(((bf16[2,512,512]{2,1,0:T(8,128)(2,1)}), bf16[64,512,512]{2,1,0:T(8,128)(2,1)}) %all-gather.2.cloned.1.call-update) | async-done | bytes 33554448 | tf_op jit(solution)/shard_map/all_gather | solution.py:149
  1757.6 6.3 gather_fusion.14
  1763.8 10.6 convert_bitcast_fusion
  (18 shorter events, 0.7 us)
Async XLA Ops:
  7.2 1750.4 %all-gather.2.cloned.1.call-start = ((), (), s32[]{:S(2)}) async-start(), calls=%async_computation | async-start | bytes 34603008 | tf_op jit(solution)/shard_map/all_gather | solution.py:149
  66.9 1621.6 %copy-start.21 = (s32[1,32]{1,0:T(1,128)S(1)}, s32[1,32]{1,0:T(1,128)}, u32[]{:S(2)}) copy-start(s32[1,32]{1,0:T(1,128)} %param.26) | copy-start | bytes 388
Sparse Core Ops, SparseCore 0:
  92.4 1665.1 all-gather.1
where the time goes:
time: 1800 us; the launch traced here: 1780 us
  blocking collectives  1580 us (88%)
  waiting for transfers between devices  68.1 us (4%)
  local copies, waits for them, and re-layouts  40.6 us (2%)
  loops' own time  39.2 us (2%)
  between operations  24.6 us (1%)
    pmax x4, blocking collectives, by_axis(): return functools.reduce(lax.pmax, axes, x)  1580 us
    all_gather x1, waiting for transfers between devices, per_device(): gathered = lax.all_gather(factors, BLK, axis=0, tiled=True)  68.1 us
    another operation x4, loops' own time, per_device(): lax.cond(active, one_sweep, keep_both, states[slot_index], eigen_bases[sl...  39.2 us
  transfers between devices with their start and end apart: 1, of which 1 were waited for; matrix products, arithmetic and copies ran while one was open for 0% of the time, Pallas kernels for 0%

commit v1 on v0

v1 whole, which is shorter than its diff:
```python
import jax
import jax.numpy as jnp
from jax import lax
from jax.experimental import pallas as pl
from jax.experimental.pallas import tpu as pltpu
from jax.sharding import Mesh
from jax.sharding import PartitionSpec as P

MAXS = 2
SIZE = 512
W = 128
PAIRINGS = ((0, 1, 2, 3), (0, 2, 1, 3), (0, 3, 1, 2))
DAMPING = 0.01
SERIES_LIMIT = 1e-4
bf16 = jnp.bfloat16
f32 = jnp.float32


def halves(x):
    high = x.astype(bf16)
    low = (x - high.astype(f32)).astype(bf16)
    return high, low


def dot3(left, right):
    lh, ll = left
    rh, rl = right
    return jnp.dot(
        jnp.concatenate([lh, ll, lh], axis=1),
        jnp.concatenate([rh, rh, rl], axis=0),
        preferred_element_type=f32,
    )


def thirds(x):
    high, _ = halves(x)
    rest = x - high.astype(f32)
    middle, low = halves(rest)
    return high, middle, low


def dot6(left, right):
    a, b, c = thirds(left)
    x, y, z = thirds(right)
    return jnp.dot(
        jnp.concatenate([a, a, b, b, a, c], axis=1),
        jnp.concatenate([x, y, x, y, z, x], axis=0),
        preferred_element_type=f32,
    )


def beside(x, y):
    return tuple(jnp.concatenate([a, b], axis=1) for a, b in zip(x, y))


def angles_of(coupling, lower, upper):
    difference = upper - lower
    total = upper + lower
    bottom = difference * difference + 4.0 * coupling * coupling + DAMPING * (total * total)
    return coupling * difference / bottom


def span(member):
    return slice(member * W, member * W + W)


def eye(size):
    return lax.broadcasted_iota(jnp.int32, (size, size), 0) == lax.broadcasted_iota(
        jnp.int32, (size, size), 1
    )


def series_half(a, at, check):
    ah, th = halves(a), halves(at)
    x = 0.25 * dot3(ah, th)
    xh = halves(x)
    both = dot3(xh, beside(xh, ah))
    x2, b1 = both[:, :W], a - both[:, W:]
    x2h = halves(x2)
    both = dot3(x2h, beside(x2h, halves(b1)))
    x4, b2 = both[:, :W], b1 + both[:, W:]
    t = b2 + dot3(halves(x4), halves(b2))
    part = x4 * x4
    part = sum(part[8 * i : 8 * i + 8] for i in range(W // 8))
    check[...] += part
    tp = halves(t)
    return t, dot3(tp, th), dot3(th, tp)


def newton_half(a, at):
    one = jnp.where(eye(W), 1.0, 0.0).astype(f32)
    s = one + 0.25 * dot6(a, at)
    norm = jnp.max(jnp.sum(jnp.abs(s), axis=1, keepdims=True), axis=0, keepdims=True)

    def step(_, y):
        return dot6(y, 2.0 * one - dot6(s, y))

    y = lax.fori_loop(0, 14, step, one * (2.0 / (1.0 + norm)))
    t = dot6(y, a)
    return t, dot6(t, at), dot6(at, t)


def one_round(m, v, rot, check, pairing, exact):
    pairs = (pairing[:2], pairing[2:])
    diagonal = eye(W)
    one = jnp.where(diagonal, 1.0, 0.0).astype(f32)
    rs, rts = [], []
    for p, q in pairs:
        dp = jnp.where(diagonal, m[span(p), span(p)], 0.0)
        dq = jnp.where(diagonal, m[span(q), span(q)], 0.0)
        row_p, row_q = (jnp.sum(d, axis=0, keepdims=True) for d in (dp, dq))
        col_p, col_q = (jnp.sum(d, axis=1, keepdims=True) for d in (dp, dq))
        a = angles_of(m[span(p), span(q)], col_p, row_q)
        at = angles_of(m[span(q), span(p)], row_p, col_q)
        t, tat, att = newton_half(a, at) if exact else series_half(a, at, check)
        tt = t.T
        r00, r11 = one - 0.5 * tat, one - 0.5 * att
        rs.append(halves(jnp.concatenate(
            [jnp.concatenate([r00, t], axis=1), jnp.concatenate([-tt, r11], axis=1)], axis=0)))
        rts.append(halves(jnp.concatenate(
            [jnp.concatenate([r00, -t], axis=1), jnp.concatenate([tt, r11], axis=1)], axis=0)))

    def load(ref, rows, cols):
        return jnp.concatenate(
            [jnp.concatenate([ref[span(i), span(j)] for j in cols], axis=1) for i in rows], axis=0)

    def store(ref, rows, cols, value):
        for x, i in enumerate(rows):
            for y, j in enumerate(cols):
                ref[span(i), span(j)] = value[x * W : x * W + W, y * W : y * W + W]

    for x, y in ((0, 1), (0, 0), (1, 1)):
        rows, cols = pairs[x], pairs[y]
        g = dot3(halves(load(m, rows, cols)), rs[y])
        new = dot3(rts[x], halves(g))
        store(m, rows, cols, new)
        if x != y:
            store(m, cols, rows, new.T)
    for h, cols in enumerate(pairs):
        for i in range(4):
            new = dot3(halves(load(v, (i,), cols)), rs[h])
            store(v, (i,), cols, new)


def roots_kernel(run_ref, stat_ref, factor_ref, peaks_ref, m, v, check, norms):
    slot = pl.program_id(0)
    sweeps = run_ref[slot]

    @pl.when(slot == 0)
    def _():
        peaks_ref[...] = jnp.zeros_like(peaks_ref)

    def start():
        m[...] = stat_ref[0]
        v[...] = jnp.where(eye(SIZE), 1.0, 0.0).astype(f32)
        check[...] = jnp.zeros_like(check)
        norms[...] = jnp.zeros_like(norms)

    def all_sweeps(exact):
        def sweep(s, carry):
            for pairing in PAIRINGS:
                one_round(m, v, None, check, pairing, exact)
            square = m[...] * m[...]
            off = jnp.sum(jnp.where(eye(SIZE), 0.0, square), axis=0, keepdims=True)
            whole = jnp.sum(square, axis=0, keepdims=True)
            off = jnp.sum(off, axis=1, keepdims=True)
            whole = jnp.sum(whole, axis=1, keepdims=True)
            here = lax.broadcasted_iota(jnp.int32, (8, W), 0) == s
            norms[...] = jnp.where(here, jnp.sqrt(off / whole), norms[...])
            return carry
        lax.fori_loop(0, sweeps, sweep, 0)

    @pl.when(sweeps > 0)
    def _():
        start()
        all_sweeps(False)
        fine = jnp.sum(check[...]) <= SERIES_LIMIT

        @pl.when(jnp.logical_not(fine))
        def _():
            start()
            all_sweeps(True)

        square = jnp.where(eye(SIZE), m[...], 0.0)
        scale = jnp.sum(square, axis=0, keepdims=True)
        scale = lax.rsqrt(jnp.sqrt(scale))
        left = halves(v[...] * scale)
        right = halves(v[...])
        for i in range(4):
            lh, ll = (part[span(i)] for part in left)
            value = lax.dot_general(
                jnp.concatenate([lh, ll, lh], axis=1),
                jnp.concatenate([right[0], right[0], right[1]], axis=1),
                (((1,), (1,)), ((), ())),
                preferred_element_type=f32,
            )
            factor_ref[0, span(i)] = value.astype(bf16)
        peaks_ref[...] = jnp.maximum(peaks_ref[...], norms[...])

    @pl.when(sweeps == 0)
    def _():
        factor_ref[...] = jnp.zeros_like(factor_ref)


def roots(run, statistics):
    slots = statistics.shape[0]
    return pl.pallas_call(
        roots_kernel,
        grid_spec=pltpu.PrefetchScalarGridSpec(
            num_scalar_prefetch=1,
            grid=(slots,),
            in_specs=[pl.BlockSpec((1, SIZE, SIZE), lambda i, run: (i, 0, 0))],
            out_specs=[
                pl.BlockSpec((1, SIZE, SIZE), lambda i, run: (i, 0, 0)),
                pl.BlockSpec((8, W), lambda i, run: (0, 0)),
            ],
            scratch_shapes=[
                pltpu.VMEM((SIZE, SIZE), f32),
                pltpu.VMEM((SIZE, SIZE), f32),
                pltpu.VMEM((8, W), f32),
                pltpu.VMEM((8, W), f32),
            ],
        ),
        out_shape=[
            jax.ShapeDtypeStruct((slots, SIZE, SIZE), bf16),
            jax.ShapeDtypeStruct((8, W), f32),
        ],
        compiler_params=pltpu.CompilerParams(dimension_semantics=("arbitrary",)),
    )(run, statistics)


BLK = ("blk_0", "blk_1", "blk_2")
BLK_GRP = ("blk_0", "blk_1", "blk_2", "grp")


def per_device(statistics, gradients, live_counts, slot_row, sweeps):
    slot_count = statistics.shape[1]
    row_count = gradients.shape[1]
    blk_rank = lax.axis_index(BLK)
    own_live = lax.dynamic_index_in_dim(live_counts[0], blk_rank, 0, keepdims=False)
    run = jnp.where(lax.iota(jnp.int32, slot_count) < own_live, sweeps[0], 0)
    factors, peaks = roots(run, statistics[0])
    off_max = peaks[:MAXS, 0]
    for axis in BLK_GRP:
        off_max = lax.pmax(off_max, axis)
    gathered = lax.all_gather(factors, BLK, axis=0, tiled=True)
    slot_total = gathered.shape[0]
    slot_ids = lax.iota(jnp.int32, slot_total)
    row_ids = lax.iota(jnp.int32, row_count)
    is_live = slot_ids % slot_count < jnp.repeat(live_counts[0], slot_count)
    matches = (slot_row[0][None, :] == row_ids[:, None]) & is_live[None, :]
    slot_of = jnp.sum(jnp.where(matches, slot_ids[None, :], 0), axis=1)
    chosen = jnp.take(gathered, slot_of, axis=0)
    updates = jnp.einsum("kij,kjc->kic", chosen, gradients[0], preferred_element_type=jnp.float32)
    return (updates.astype(jnp.bfloat16)[None], off_max)


def solution(mesh):
    split = Mesh(
        mesh.devices.reshape(4, 4, 2, mesh.shape["grp"]), ("blk_0", "blk_1", "blk_2", "grp")
    )
    return jax.shard_map(
        per_device,
        mesh=split,
        in_specs=(
            P("grp", BLK, None, None),
            P("grp", None, None, BLK),
            P("grp", None),
            P("grp", None),
            P("grp", BLK),
        ),
        out_specs=(P("grp", None, None, BLK), P()),
        check_vma=False,
    )
```

time: 1800 us -> 370 us (0.21); the launches traced: 1780 us -> 371 us
  blocking collectives: 1580 us -> 192 us
  Pallas kernels: 0 us -> 58.4 us
  loops' own time: 39.2 us -> 0 us
  local copies, waits for them, and re-layouts: 40.6 us -> 9.12 us
    pmax x4, blocking collectives: 1580 us -> 192 us  [per_device(): off_max = lax.pmax(off_max, axis)]
    pallas_call x0 -> x1, Pallas kernels: none -> 58.4 us  [roots(): pl.pallas_call(roots_kernel, grid_spec=pltpu.PrefetchScalarGridSpec(num_s...]
    another operation x4 -> x0, loops' own time: 39.2 us -> none  [per_device(): lax.cond(active, one_sweep, keep_both, states[slot_index], eigen_bases[sl...]
  transfers between devices with their start and end apart: 1 -> 1, of which waited for: 1 -> 1; matrix products, arithmetic and copies ran while one was open for 0% -> 1% of each run, Pallas kernels for 0% -> 0%
where the time goes in v1:
time: 370 us; the launch traced here: 371 us
  blocking collectives  192 us (52%)
  waiting for transfers between devices  83.7 us (23%)
  Pallas kernels  58.4 us (16%)
  between operations  14.1 us (4%)
  matrix products  10.6 us (3%)
  local copies, waits for them, and re-layouts  9.12 us (2%)
    pmax x4, blocking collectives, per_device(): off_max = lax.pmax(off_max, axis)  192 us
    all_gather x1, waiting for transfers between devices, per_device(): gathered = lax.all_gather(factors, BLK, axis=0, tiled=True)  83.7 us
    pallas_call x1, Pallas kernels, roots(): pl.pallas_call(roots_kernel, grid_spec=pltpu.PrefetchScalarGridSpec(num_s...  58.4 us
    dot_general x1, matrix products, per_device(): jnp.einsum('kij,kjc->kic', chosen, gradients[0], preferred_element_type=j...  10.6 us
  transfers between devices with their start and end apart: 1, of which 1 were waited for; matrix products, arithmetic and copies ran while one was open for 1% of the time, Pallas kernels for 0%

profile of v1, /device:TPU:1, one launch (start us, length us, event | category | flops | bytes accessed | tf_op | source)
XLA Modules:
  0.0 371.0 jit_solution(10053838667289882251)
XLA Ops:
  7.2 0.0 all-gather.2.cloned.1.call-start
  7.2 1.2 constant_dynamic-slice_fusion
  8.5 1.9 compare_select_fusion.2.run_ref
  10.4 58.4 %shard_map.68 = (bf16[2,512,512]{2,1,0:T(8,128)(2,1)}, f32[8,128]{1,0:T(8,128)}) custom-call(s32[2]{0:T(128)} %compare_select_fusion.2.run_ref, f32[2,512,512]{2,1,0:T(8,128)} %bitcast.17), custom_call_target="tpu_custom_call" | custom-call | tf_op jit(solution)/shard_map/pallas_call | solution.py:207
  68.8 0.0 all-gather.2.cloned.1.call-update
  68.8 0.8 slice_reduce_fusion
  69.6 6.0 %pmax.28 = f32[2]{0:T(128)S(1)} all-reduce(f32[2]{0:T(128)S(1)} %slice_reduce_fusion), channel_id=1, replica_groups=mesh['blk_0'=4,'blk_1'=4,'blk_2'=2,'grp'=4] {'blk_0'}, use_global_device_ids=true, to_apply=%region_1.2 | all-reduce | flops 2 | bytes 16 | tf_op jit(solution)/shard_map/pmax | solution.py:245
  75.6 172.7 %pmax.29 = f32[2]{0:T(128)S(1)} all-reduce(f32[2]{0:T(128)S(1)} %pmax.28), channel_id=1, replica_groups=mesh['blk_0'=4,'blk_1'=4,'blk_2'=2,'grp'=4] {'blk_1'}, use_global_device_ids=true, to_apply=%region_2.3 | all-reduce | flops 2 | bytes 16 | tf_op jit(solution)/shard_map/pmax | solution.py:245
  248.3 2.5 pmax.30
  250.7 11.3 %pmax.31 = f32[2]{0:T(128)} all-reduce(f32[2]{0:T(128)S(1)} %pmax.30), channel_id=1, replica_groups=mesh['blk_0'=4,'blk_1'=4,'blk_2'=2,'grp'=4] {'grp'}, use_global_device_ids=true, to_apply=%region_4.5 | all-reduce | flops 2 | bytes 16 | tf_op jit(solution)/shard_map/pmax | solution.py:245
  262.0 0.7 broadcast_in_dim.35
  262.7 0.1 reshape.41
  262.8 0.8 select_reduce_fusion
  263.6 83.7 %all-gather.2.cloned.1.call-done = bf16[64,512,512]{2,1,0:T(8,128)(2,1)} async-done(((bf16[2,512,512]{2,1,0:T(8,128)(2,1)}), bf16[64,512,512]{2,1,0:T(8,128)(2,1)}) %all-gather.2.cloned.1.call-update) | async-done | bytes 33554448 | tf_op jit(solution)/shard_map/all_gather | solution.py:246
  347.3 6.3 %gather_fusion = bf16[16,512,512]{2,1,0:T(8,128)(2,1)} fusion(bf16[64,512,512]{2,1,0:T(8,128)(2,1)} %all-gather.2.cloned.1.call-done, s32[1024]{0:T(1024)S(1)} %pad_clamp_fusion), kind=kCustom, calls=%fused_computation | custom fusion | bytes 16777280 | tf_op jit(solution)/shard_map/jit(_take)/gather | solution.py:253
  353.6 10.6 %convert_bitcast_fusion = bf16[1,16,512,448]{2,3,1,0:T(8,128)(2,1)} fusion(bf16[1,16,512,448]{2,3,1,0:T(8,128)(2,1)} %param.6, bf16[16,512,512]{2,1,0:T(8,128)(2,1)} %gather_fusion, pred[16]{0:T(512)(128)(4,1)S(1)} %compare_and_fusion), kind=kOutput, calls=%fused_computation.5 | convolution fusion | flops 3765960704 | bytes 23068688 | tf_op jit(solution)/shard_map/kij,kjc->kic/dot_general | solution.py:254
  (4 shorter events, 0.0 us)
Async XLA Ops:
  7.2 340.2 %all-gather.2.cloned.1.call-start = ((), (), s32[]{:S(2)}) async-start(), calls=%async_computation | async-start | bytes 34603008 | tf_op jit(solution)/shard_map/all_gather | solution.py:246
Sparse Core Ops, SparseCore 0:
  68.9 278.3 all-gather.1
